TPU v7x, 256 devices: a whole 4x4x8 slice. The times are simulated.
256 devices in a mesh: blk: 64 (over z, y, x_hi), batch: 4 (over x_lo, core).
Axes of the slice: x: 4 (x_hi: 2, x_lo: 2; x = x_hi * 2 + x_lo), y: 4, z: 8, core: 2. Of those that a mesh axis runs over, the one named last changes fastest.
Arguments:
- coefficients: bfloat16 [120, 196608], P(None, ('blk', 'batch')), may hold values from -6 to 6
- transforms: bfloat16 [12, 24, 196608], P(None, 'batch', 'blk'), may hold values from -6 to 6
- basis: bfloat16 [120, 3, 32768], P(None, None, 'blk'), may hold values from -0.5 to 0.5
- template: bfloat16 [3, 32768], P(None, 'blk'), may hold values from -6 to 6
- skin_weights: bfloat16 [24, 32768], P(None, 'blk'), may hold values from 0.019897461 to 1
Outputs:
- skinned: bfloat16 [196608, 4, 3, 512], P(('blk', 'batch'))
All inputs are finite; a program needn't handle non-finite values.
Results may differ from a plain program's by a relative error of at most 0.0049.
Values may be sent and summed in bfloat16 or wider, within the bound.
A program may use at most 192 MiB of HBM per device.

v0:
```python
import jax
import jax.numpy as jnp
from jax import lax
from jax.sharding import Mesh
from jax.sharding import PartitionSpec as P

STEPS = 4
BATCH = ("batch_0", "batch_1")
BLK_BATCH = ("blk", "batch_0", "batch_1")


def cut_along(x, dim, count):
    dims = x.shape
    blocks = x.reshape(*dims[:dim], count, dims[dim] // count, *dims[dim + 1 :])
    return jnp.moveaxis(blocks, dim, 0)


def joined_along(blocks, dim):
    dims = list(blocks.shape[1:])
    dims[dim] *= blocks.shape[0]
    return jnp.moveaxis(blocks, 0, dim).reshape(dims)


def moved_by_axis(blocks, axes, turns):
    inside = blocks.shape[1:]
    out = blocks.reshape(*(lax.axis_size(a) for a in axes), *inside)
    for k in turns:
        out = lax.all_to_all(out, axes[k], k, k, tiled=True)
    return out.reshape(-1, *inside)


def exchange_by_chip(x, groups, turns, split_dim, concat_dim):
    count = lax.axis_size(groups[0]) * lax.axis_size(groups[1])
    blocks = cut_along(x, split_dim, count)
    return joined_along(moved_by_axis(blocks, groups, turns), concat_dim)


def as_sent(x):
    return jax.tree.map(lambda a: a.astype(jnp.bfloat16) if a.dtype == jnp.float32 else a, x)


def passed_along(block, axis, distance):
    devices = range(lax.axis_size(axis))
    route = [((i - distance) % len(devices), i) for i in devices]
    return lax.ppermute(block, axis, route)


def skin_block(coefficients, joint_poses, basis_block, template_block, weight_block):
    flattened = basis_block.reshape(basis_block.shape[0], -1)
    shaped = lax.dot_general(
        coefficients, flattened, (((0,), (0,)), ((), ())), preferred_element_type=jnp.float32
    )
    shaped = shaped + template_block.reshape(1, -1).astype(jnp.float32)
    shaped = shaped.reshape(coefficients.shape[1], 3, -1)
    blended = jnp.einsum(
        "mjr,jv->mrv", joint_poses, weight_block, preferred_element_type=jnp.float32
    )
    positions = []
    for matrix_row in range(3):
        component = blended[4 * matrix_row + 3]
        for column in range(3):
            component = component + blended[4 * matrix_row + column] * shaped[:, column, :]
        positions.append(component)
    return jnp.stack(positions, axis=1).astype(jnp.bfloat16)


def normalize(skin_weights):
    weight_float = skin_weights.astype(jnp.float32)
    return (weight_float / jnp.sum(weight_float, axis=0, keepdims=True)).astype(jnp.bfloat16)


def per_device(coefficients, transforms, basis, template, skin_weights):
    normalized = normalize(skin_weights)
    joint_poses = exchange_by_chip(transforms, ("batch_0", "batch_1"), (1, 0), 2, 1)
    resident = (basis, template, normalized)
    stacked = tuple((member[None] for member in resident))
    covered = 1
    while covered < STEPS:
        shifted = jax.tree.map(
            lambda part, own: part.astype(own.dtype),
            passed_along(as_sent(stacked), "blk", covered),
            stacked,
        )
        stacked = tuple(
            (
                jnp.concatenate([current, arrived], axis=0)
                for current, arrived in zip(stacked, shifted)
            )
        )
        covered = covered * 2
    sources = [tuple((member[slot_index] for member in stacked)) for slot_index in range(STEPS)]
    outputs = [
        skin_block(coefficients, joint_poses, source[0], source[1], source[2]) for source in sources
    ]
    return jnp.stack(outputs, axis=1)


def solution(mesh):
    split = Mesh(mesh.devices.reshape(mesh.shape["blk"], 2, 2), ("blk", "batch_0", "batch_1"))
    in_specs = (
        P(None, BLK_BATCH),
        P(None, BATCH, "blk"),
        P(None, None, "blk"),
        P(None, "blk"),
        P(None, "blk"),
    )
    out_specs = P(BLK_BATCH, None, None, None)
    return jax.shard_map(
        per_device, mesh=split, in_specs=in_specs, out_specs=out_specs, check_vma=False
    )
```

profile of v0, /device:TPU:126, one launch (start us, length us, event | category | flops | bytes accessed | tf_op | source)
XLA Modules:
  0.0 139.9 jit_solution(4334563824386905580)
XLA Ops:
  0.0 3.6 %collective-permute-start.2 = (bf16[1,3,512]{2,1,0:T(4,128)(2,1)}, bf16[1,3,512]{2,1,0:T(4,128)(2,1)S(1)}, u32[]{:S(2)}, u32[]{:S(2)}) collective-permute-start(bf16[1,3,512]{2,1,0:T(4,128)(2,1)} %bitcast.533), channel_id=1, source_target_pairs={{252,0},{0,4},{4,8},{8,12},{12,16},{16,20},{20,24},{24,28},{28,32}... | collective-permute-start | bytes 9224 | tf_op jit(solution)/shard_map/ppermute | solution.py:45
  3.6 0.8 convert_reduce_fusion
  4.4 0.7 fusion.99
  5.1 2.2 %collective-permute-start = (bf16[1,24,512]{2,1,0:T(8,128)(2,1)S(1)}, bf16[1,24,512]{2,1,0:T(8,128)(2,1)S(1)}, u32[]{:S(2)}, u32[]{:S(2)}) collective-permute-start(bf16[1,24,512]{2,1,0:T(8,128)(2,1)S(1)} %fusion.99), channel_id=1, source_target_pairs={{252,0},{0,4},{4,8},{8,12},{12,16},{16,20},{20,24},{24,28},{28,32}... | collective-permute-start | bytes 73736 | tf_op jit(solution)/shard_map/ppermute | solution.py:45
  7.3 1.4 reshape.289
  8.7 0.2 reshape.290
  8.9 0.3 copy.26
  9.3 4.1 %all_to_all.10 = bf16[2,2,12,6,768]{4,0,3,2,1:T(2,128)(2,1)S(1)} all-to-all(bf16[2,2,12,6,768]{4,0,3,2,1:T(2,128)(2,1)S(1)} %copy.26), channel_id=1, replica_groups=mesh['blk'=64,'batch_0'=2,'batch_1'=2] {'batch_1'}, dimensions={1} | all-to-all | bytes 884736 | tf_op jit(solution)/shard_map/all_to_all | solution.py:28
  13.3 1.1 copy.27
  14.4 4.3 %all-to-all-start.1 = ((bf16[2,2,12,6,768]{4,1,3,2,0:T(2,128)(2,1)}), bf16[2,2,12,6,768]{4,1,3,2,0:T(2,128)(2,1)S(1)}, u32[]{:S(2)}, u32[]{:S(2)}) async-start(bf16[2,2,12,6,768]{4,1,3,2,0:T(2,128)(2,1)} %copy.27), calls=%async_computation.1 | async-start | bytes 884736 | tf_op jit(solution)/shard_map/all_to_all | solution.py:28
  18.7 2.1 %collective-permute-start.1 = (bf16[1,120,3,512]{3,1,2,0:T(8,128)(2,1)S(1)}, bf16[1,120,3,512]{3,1,2,0:T(8,128)(2,1)S(1)}, u32[]{:S(2)}, u32[]{:S(2)}) collective-permute-start(bf16[1,120,3,512]{3,1,2,0:T(8,128)(2,1)S(1)} %bitcast.531), channel_id=1, source_target_pairs={{252,0},{0,4},{4,8},{8,12},{12,16},{16,20},{20,24},{24,28},{28,32}... | collective-permute-start | bytes 1105928 | tf_op jit(solution)/shard_map/ppermute | solution.py:45
  20.9 0.2 copy.30
  21.1 1.7 %collective-permute-start.5 = (bf16[2,3,512]{2,1,0:T(4,128)(2,1)S(1)}, bf16[2,3,512]{2,1,0:T(4,128)(2,1)S(1)}, u32[]{:S(2)}, u32[]{:S(2)}) collective-permute-start(bf16[2,3,512]{2,1,0:T(4,128)(2,1)S(1)} %pad_maximum_fusion.2), channel_id=1, source_target_pairs={{248,0},{252,4},{0,8},{4,12},{8,16},{12,20},{16,24},{20,28},{24,32... | collective-permute-start | bytes 18440 | tf_op jit(solution)/shard_map/ppermute | solution.py:45
  22.8 3.0 %convolution_add_fusion.3 = f32[768,1536]{1,0:T(8,128)} fusion(bf16[120,768]{1,0:T(8,128)(2,1)S(1)} %copy-done, bf16[120,1536]{0,1:T(8,128)(2,1)S(1)} %bitcast.527, f32[1536]{0:T(1024)S(1)} %reshape.297), kind=kOutput, calls=%fused_computation.8 | convolution fusion | flops 284295168 | bytes 5277696 | tf_op jit(solution)/shard_map/dot_general | solution.py:50
  25.8 6.0 %copy.31 = f32[768,1536]{0,1:T(8,128)} copy(f32[768,1536]{1,0:T(8,128)} %convolution_add_fusion.3) | data formatting | bytes 9437184 | tf_op jit(solution)/shard_map/add | solution.py:53
  31.9 3.2 %collective-permute-start.3 = (bf16[2,24,512]{2,1,0:T(8,128)(2,1)S(1)}, bf16[2,24,512]{2,1,0:T(8,128)(2,1)S(1)}, u32[]{:S(2)}, u32[]{:S(2)}) collective-permute-start(bf16[2,24,512]{2,1,0:T(8,128)(2,1)S(1)} %pad_maximum_fusion.1), channel_id=1, source_target_pairs={{248,0},{252,4},{0,8},{4,12},{8,16},{12,20},{16,24},{20,28},{24,32... | collective-permute-start | bytes 147464 | tf_op jit(solution)/shard_map/ppermute | solution.py:45
  35.1 0.3 copy.28
  35.4 0.2 reshape.291
  35.8 0.3 copy-done.10
  36.2 2.7 %convolution_bitcast_fusion.3 = f32[12,768,512]{1,2,0:T(8,128)S(1)} fusion(bf16[12,24,768]{2,1,0:T(8,128)(2,1)S(1)} %reshape.292, bf16[24,512]{1,0:T(8,128)(2,1)S(1)} %copy-done.10, f32[512]{0:T(512)S(1)} %convert_reduce_fusion), kind=kOutput, calls=%fused_computation.4 | convolution fusion | flops 226529280 | bytes 19343360 | tf_op jit(solution)/shard_map/mjr,jv->mrv/dot_general | solution.py:55
  38.8 8.1 %convolution_bitcast_fusion = f32[12,768,512]{1,2,0:T(8,128)} fusion(bf16[12,24,768]{2,1,0:T(8,128)(2,1)S(1)} %reshape.292, bf16[2,24,512]{2,1,0:T(8,128)(2,1)S(1)} %collective-permute-done.3), kind=kOutput, calls=%fused_computation.1 | convolution fusion | flops 226492416 | bytes 19341312 | tf_op jit(solution)/shard_map/mjr,jv->mrv/dot_general | solution.py:55
  46.9 8.1 %convolution_bitcast_fusion.1 = f32[12,768,512]{1,2,0:T(8,128)} fusion(bf16[12,24,768]{2,1,0:T(8,128)(2,1)S(1)} %reshape.292, bf16[2,24,512]{2,1,0:T(8,128)(2,1)S(1)} %collective-permute-done.3), kind=kOutput, calls=%fused_computation.2 | convolution fusion | flops 226492416 | bytes 19341312 | tf_op jit(solution)/shard_map/mjr,jv->mrv/dot_general | solution.py:55
  55.0 8.0 %convolution_bitcast_fusion.2 = f32[12,768,512]{1,2,0:T(8,128)} fusion(bf16[12,24,768]{2,1,0:T(8,128)(2,1)S(1)} %reshape.292, bf16[1,24,512]{2,1,0:T(8,128)(2,1)S(1)} %collective-permute-done), kind=kOutput, calls=%fused_computation.3 | convolution fusion | flops 226492416 | bytes 19341312 | tf_op jit(solution)/shard_map/mjr,jv->mrv/dot_general | solution.py:55
  63.0 1.1 fusion.84
  64.2 1.5 %fusion.86 = bf16[768,1,1,512]{0,3,2,1:T(8,128)(2,1)} fusion(f32[768,3,512]{0,2,1:T(8,128)S(1)} %bitcast.518, f32[12,768,512]{1,2,0:T(8,128)S(1)} %convolution_bitcast_fusion.3), kind=kLoop, calls=%fused_computation.143 | loop fusion | flops 2752512 | bytes 11796480 | tf_op jit(solution)/shard_map/stack | solution.py:64
  65.7 1.0 pad_maximum_fusion
  66.6 3.7 %collective-permute-start.4 = (bf16[2,120,3,512]{3,1,2,0:T(8,128)(2,1)}, bf16[2,120,3,512]{3,1,2,0:T(8,128)(2,1)}, u32[]{:S(2)}, u32[]{:S(2)}) collective-permute-start(bf16[2,120,3,512]{3,1,2,0:T(8,128)(2,1)} %pad_maximum_fusion), channel_id=1, source_target_pairs={{248,0},{252,4},{0,8},{4,12},{8,16},{12,20},{16,24},{20,28},{24,32... | collective-permute-start | bytes 2211848 | tf_op jit(solution)/shard_map/ppermute | solution.py:45
  70.3 0.2 copy.32
  70.5 3.0 %convolution_add_fusion.2 = f32[768,1536]{1,0:T(8,128)} fusion(bf16[120,768]{1,0:T(8,128)(2,1)S(1)} %copy-done, bf16[120,1536]{0,1:T(8,128)(2,1)S(1)} %bitcast.530, f32[1536]{0:T(1024)S(1)} %reshape.298), kind=kOutput, calls=%fused_computation.7 | convolution fusion | flops 284295168 | bytes 5277696 | tf_op jit(solution)/shard_map/dot_general | solution.py:50
  73.5 6.0 %copy.33 = f32[768,1536]{0,1:T(8,128)} copy(f32[768,1536]{1,0:T(8,128)} %convolution_add_fusion.2) | data formatting | bytes 9437184 | tf_op jit(solution)/shard_map/add | solution.py:53
  79.6 5.8 %fusion.89 = bf16[768,1,1,512]{0,3,2,1:T(8,128)(2,1)} fusion(f32[768,3,512]{0,2,1:T(8,128)} %bitcast.523, f32[12,768,512]{1,2,0:T(8,128)} %convolution_bitcast_fusion.2), kind=kLoop, calls=%fused_computation.146 | loop fusion | flops 2752512 | bytes 11796480 | tf_op jit(solution)/shard_map/stack | solution.py:64
  85.4 5.3 %fusion.87 = (bf16[768,1,1,512]{0,3,2,1:T(8,128)(2,1)S(1)}, bf16[768,1,1,512]{0,3,2,1:T(8,128)(2,1)S(1)}) fusion(f32[768,3,512]{0,2,1:T(8,128)S(1)} %bitcast.524, f32[12,768,512]{1,2,0:T(8,128)} %convolution_bitcast_fusion.2), kind=kLoop, calls=%fused_computation.144 | loop fusion | flops 5505024 | bytes 18874368 | tf_op jit(solution)/shard_map/stack | solution.py:64
  90.7 2.0 %fusion.101 = (bf16[1,120,3,512]{3,1,2,0:T(8,128)(2,1)}, bf16[1,120,3,512]{3,1,2,0:T(8,128)(2,1)}) fusion(bf16[2,120,3,512]{3,1,2,0:T(8,128)(2,1)} %collective-permute-done.4), kind=kLoop, calls=%fused_computation.166 | loop fusion | bytes 1474560 | tf_op jit(solution)/shard_map/slice | solution.py:91
  92.8 1.9 %copy.34 = bf16[1,120,3,512]{1,3,2,0:T(8,128)(2,1)} copy(bf16[1,120,3,512]{3,1,2,0:T(8,128)(2,1)} %get-tuple-element.13) | data formatting | bytes 737280 | tf_op jit(solution)/shard_map/slice | solution.py:91
  94.7 1.9 %copy.35 = bf16[1,120,3,512]{1,3,2,0:T(8,128)(2,1)} copy(bf16[1,120,3,512]{3,1,2,0:T(8,128)(2,1)} %get-tuple-element.14) | data formatting | bytes 737280 | tf_op jit(solution)/shard_map/slice | solution.py:91
  96.6 1.8 %convolution_add_fusion.1 = f32[1536,768]{1,0:T(8,128)S(1)} fusion(bf16[120,1536]{0,1:T(8,128)(2,1)} %bitcast.528, bf16[120,768]{1,0:T(8,128)(2,1)S(1)} %copy-done, f32[1536]{0:T(1024)S(1)} %reshape.299), kind=kOutput, calls=%fused_computation.6 | convolution fusion | flops 284295168 | bytes 5277696 | tf_op jit(solution)/shard_map/dot_general | solution.py:50
  98.4 0.8 convolution_add_fusion
  99.3 6.6 %fusion.90 = (bf16[768,1,1,512]{0,3,2,1:T(8,128)(2,1)}, bf16[768,1,1,512]{0,3,2,1:T(8,128)(2,1)}) fusion(f32[768,3,512]{0,2,1:T(8,128)S(1)} %bitcast.521, f32[12,768,512]{1,2,0:T(8,128)} %convolution_bitcast_fusion.1), kind=kLoop, calls=%fused_computation.147 | loop fusion | flops 5505024 | bytes 18874368 | tf_op jit(solution)/shard_map/stack | solution.py:64
  105.9 7.3 %fusion.92 = (bf16[768,1,1,512]{0,3,2,1:T(8,128)(2,1)}, bf16[768,1,1,512]{0,3,2,1:T(8,128)(2,1)}) fusion(f32[768,3,512]{0,2,1:T(8,128)S(1)} %bitcast.522, f32[12,768,512]{1,2,0:T(8,128)} %convolution_bitcast_fusion.1, f32[768,3,512]{0,2,1:T(8,128)S(1)} %bitcast.519, f32[12,768,512]{1,2,0:T(8,128)} %convolution_bitcast_fusion), kind=kLoop, calls=%fused_computation.149 | loop fusion | flops 5505024 | bytes 23592960 | tf_op jit(solution)/shard_map/stack | solution.py:64
  113.2 0.2 slice-done.3
  113.5 0.9 slice-done.4
  114.4 1.2 fusion.93
  115.7 0.2 copy-done.4
  116.0 0.2 copy-done.5
  116.2 0.2 copy-done.6
  116.5 0.2 copy-done.7
  116.7 6.7 %maximum_maximum_fusion = bf16[768,4,3,512]{0,3,2,1:T(8,128)(2,1)} fusion(bf16[768,1,1,512]{0,3,2,1:T(8,128)(2,1)S(1)} %copy-done.5, bf16[768,1,1,512]{0,3,2,1:T(8,128)(2,1)S(1)} %get-tuple-element.12, bf16[768,1,1,512]{0,3,2,1:T(8,128)(2,1)S(1)} %get-tuple-element.11, bf16[768,1,1,512]{0,3,2,1:T(8,128)(2,1)S(1)} %copy-done.4, ...), kind=kLoop, calls=%fused_computation | loop fusion | flops 51904512 | bytes 18874368 | tf_op jit(solution)/shard_map/stack | solution.py:95
  123.4 16.5 %copy.36 = bf16[768,4,3,512]{3,1,2,0:T(4,128)(2,1)} copy(bf16[768,4,3,512]{0,3,2,1:T(8,128)(2,1)} %maximum_maximum_fusion) | data formatting | bytes 18874368 | tf_op jit(solution)/shard_map/stack | solution.py:95
  (49 shorter events, 0.5 us)
Async XLA Ops:
  0.0 22.8 %copy-start = (bf16[120,768]{1,0:T(8,128)(2,1)S(1)}, bf16[120,768]{1,0:T(8,128)(2,1)}, u32[]{:S(2)}) copy-start(bf16[120,768]{1,0:T(8,128)(2,1)} %param.5) | copy-start | bytes 552964
  0.0 21.1 %collective-permute-start.2 = (bf16[1,3,512]{2,1,0:T(4,128)(2,1)}, bf16[1,3,512]{2,1,0:T(4,128)(2,1)S(1)}, u32[]{:S(2)}, u32[]{:S(2)}) collective-permute-start(bf16[1,3,512]{2,1,0:T(4,128)(2,1)} %bitcast.533), channel_id=1, source_target_pairs={{252,0},{0,4},{4,8},{8,12},{12,16},{16,20},{20,24},{24,28},{28,32}... | collective-permute-start | bytes 9224 | tf_op jit(solution)/shard_map/ppermute | solution.py:45
  5.1 26.8 %collective-permute-start = (bf16[1,24,512]{2,1,0:T(8,128)(2,1)S(1)}, bf16[1,24,512]{2,1,0:T(8,128)(2,1)S(1)}, u32[]{:S(2)}, u32[]{:S(2)}) collective-permute-start(bf16[1,24,512]{2,1,0:T(8,128)(2,1)S(1)} %fusion.99), channel_id=1, source_target_pairs={{252,0},{0,4},{4,8},{8,12},{12,16},{16,20},{20,24},{24,28},{28,32}... | collective-permute-start | bytes 73736 | tf_op jit(solution)/shard_map/ppermute | solution.py:45
  8.9 9.9 %copy-start.9 = (bf16[120,3,512]{2,0,1:T(8,128)(2,1)S(1)}, bf16[120,3,512]{2,0,1:T(8,128)(2,1)}, u32[]{:S(2)}) copy-start(bf16[120,3,512]{2,0,1:T(8,128)(2,1)} %param.7) | copy-start | bytes 1105924
  9.3 11.8 %copy-start.11 = (bf16[3,512]{1,0:T(4,128)(2,1)S(1)}, bf16[3,512]{1,0:T(4,128)(2,1)}, u32[]{:S(2)}) copy-start(bf16[3,512]{1,0:T(4,128)(2,1)} %param.8) | copy-start | bytes 9220
  14.4 20.7 %all-to-all-start.1 = ((bf16[2,2,12,6,768]{4,1,3,2,0:T(2,128)(2,1)}), bf16[2,2,12,6,768]{4,1,3,2,0:T(2,128)(2,1)S(1)}, u32[]{:S(2)}, u32[]{:S(2)}) async-start(bf16[2,2,12,6,768]{4,1,3,2,0:T(2,128)(2,1)} %copy.27), calls=%async_computation.1 | async-start | bytes 884736 | tf_op jit(solution)/shard_map/all_to_all | solution.py:28
  18.7 46.9 %collective-permute-start.1 = (bf16[1,120,3,512]{3,1,2,0:T(8,128)(2,1)S(1)}, bf16[1,120,3,512]{3,1,2,0:T(8,128)(2,1)S(1)}, u32[]{:S(2)}, u32[]{:S(2)}) collective-permute-start(bf16[1,120,3,512]{3,1,2,0:T(8,128)(2,1)S(1)} %bitcast.531), channel_id=1, source_target_pairs={{252,0},{0,4},{4,8},{8,12},{12,16},{16,20},{20,24},{24,28},{28,32}... | collective-permute-start | bytes 1105928 | tf_op jit(solution)/shard_map/ppermute | solution.py:45
  21.1 10.7 %collective-permute-start.5 = (bf16[2,3,512]{2,1,0:T(4,128)(2,1)S(1)}, bf16[2,3,512]{2,1,0:T(4,128)(2,1)S(1)}, u32[]{:S(2)}, u32[]{:S(2)}) collective-permute-start(bf16[2,3,512]{2,1,0:T(4,128)(2,1)S(1)} %pad_maximum_fusion.2), channel_id=1, source_target_pairs={{248,0},{252,4},{0,8},{4,12},{8,16},{12,20},{16,24},{20,28},{24,32... | collective-permute-start | bytes 18440 | tf_op jit(solution)/shard_map/ppermute | solution.py:45
  31.9 6.9 %collective-permute-start.3 = (bf16[2,24,512]{2,1,0:T(8,128)(2,1)S(1)}, bf16[2,24,512]{2,1,0:T(8,128)(2,1)S(1)}, u32[]{:S(2)}, u32[]{:S(2)}) collective-permute-start(bf16[2,24,512]{2,1,0:T(8,128)(2,1)S(1)} %pad_maximum_fusion.1), channel_id=1, source_target_pairs={{248,0},{252,4},{0,8},{4,12},{8,16},{12,20},{16,24},{20,28},{24,32... | collective-permute-start | bytes 147464 | tf_op jit(solution)/shard_map/ppermute | solution.py:45
  35.4 0.7 copy-start.10
  46.9 16.1 %slice-start.5 = ((s8[4718592]{0:T(1024)(128)(4,1)}), s8[4194304]{0:T(1024)(128)(4,1)S(1)}, s32[]{:S(2)}) async-start(s8[4718592]{0:T(1024)(128)(4,1)} %bitcast.515), calls=%async_computation.7 | async-start | bytes 8388608
  55.0 8.0 %slice-start.6 = ((s8[4718592]{0:T(1024)(128)(4,1)}), s8[524288]{0:T(1024)(128)(4,1)S(1)}, s32[]{:S(2)}) async-start(s8[4718592]{0:T(1024)(128)(4,1)} %bitcast.515), calls=%async_computation.8 | async-start | bytes 1048576
  66.6 24.1 %collective-permute-start.4 = (bf16[2,120,3,512]{3,1,2,0:T(8,128)(2,1)}, bf16[2,120,3,512]{3,1,2,0:T(8,128)(2,1)}, u32[]{:S(2)}, u32[]{:S(2)}) collective-permute-start(bf16[2,120,3,512]{3,1,2,0:T(8,128)(2,1)} %pad_maximum_fusion), channel_id=1, source_target_pairs={{248,0},{252,4},{0,8},{4,12},{8,16},{12,20},{16,24},{20,28},{24,32... | collective-permute-start | bytes 2211848 | tf_op jit(solution)/shard_map/ppermute | solution.py:45
  79.6 5.8 %copy-start.1 = (f32[768,1536]{0,1:T(8,128)S(1)}, f32[768,1536]{0,1:T(8,128)}, u32[]{:S(2)}) copy-start(f32[768,1536]{0,1:T(8,128)} %copy.33) | copy-start | bytes 14155780
  96.6 1.8 %copy-start.8 = (bf16[1,120,3,512]{1,3,2,0:T(8,128)(2,1)S(1)}, bf16[1,120,3,512]{1,3,2,0:T(8,128)(2,1)}, u32[]{:S(2)}) copy-start(bf16[1,120,3,512]{1,3,2,0:T(8,128)(2,1)} %copy.35) | copy-start | bytes 1105924
  99.2 14.0 %slice-start = ((s8[18874368]{0:T(1024)(128)(4,1)}), s8[4194304]{0:T(1024)(128)(4,1)S(1)}, s32[]{:S(2)}) async-start(s8[18874368]{0:T(1024)(128)(4,1)} %bitcast.513), calls=%async_computation.2 | async-start | bytes 8388608
  99.2 14.0 %slice-start.1 = ((s8[18874368]{0:T(1024)(128)(4,1)}), s8[4194304]{0:T(1024)(128)(4,1)S(1)}, s32[]{:S(2)}) async-start(s8[18874368]{0:T(1024)(128)(4,1)} %bitcast.513), calls=%async_computation.3 | async-start | bytes 8388608
  99.2 14.0 %slice-start.2 = ((s8[18874368]{0:T(1024)(128)(4,1)}), s8[4194304]{0:T(1024)(128)(4,1)S(1)}, s32[]{:S(2)}) async-start(s8[18874368]{0:T(1024)(128)(4,1)} %bitcast.513), calls=%async_computation.4 | async-start | bytes 8388608
  105.9 7.6 %slice-start.3 = ((s8[18874368]{0:T(1024)(128)(4,1)}), s8[4194304]{0:T(1024)(128)(4,1)S(1)}, s32[]{:S(2)}) async-start(s8[18874368]{0:T(1024)(128)(4,1)} %bitcast.513), calls=%async_computation.5 | async-start | bytes 8388608
  105.9 8.5 %slice-start.4 = ((s8[18874368]{0:T(1024)(128)(4,1)}), s8[2097152]{0:T(1024)(128)(4,1)S(1)}, s32[]{:S(2)}) async-start(s8[18874368]{0:T(1024)(128)(4,1)} %bitcast.513), calls=%async_computation.6 | async-start | bytes 4194304
  114.4 1.2 copy-start.2
  114.4 1.4 copy-start.3
  114.4 1.6 %copy-start.4 = (bf16[768,1,1,512]{0,3,2,1:T(8,128)(2,1)S(1)}, bf16[768,1,1,512]{0,3,2,1:T(8,128)(2,1)}, u32[]{:S(2)}) copy-start(bf16[768,1,1,512]{0,3,2,1:T(8,128)(2,1)} %get-tuple-element.17) | copy-start | bytes 2359300
  114.4 1.8 %copy-start.5 = (bf16[768,1,1,512]{0,3,2,1:T(8,128)(2,1)S(1)}, bf16[768,1,1,512]{0,3,2,1:T(8,128)(2,1)}, u32[]{:S(2)}) copy-start(bf16[768,1,1,512]{0,3,2,1:T(8,128)(2,1)} %get-tuple-element.18) | copy-start | bytes 2359300
  114.4 2.1 %copy-start.6 = (bf16[768,1,1,512]{0,3,2,1:T(8,128)(2,1)S(1)}, bf16[768,1,1,512]{0,3,2,1:T(8,128)(2,1)}, u32[]{:S(2)}) copy-start(bf16[768,1,1,512]{0,3,2,1:T(8,128)(2,1)} %fusion.86) | copy-start | bytes 2359300
  114.4 2.3 %copy-start.7 = (bf16[768,1,1,512]{0,3,2,1:T(8,128)(2,1)S(1)}, bf16[768,1,1,512]{0,3,2,1:T(8,128)(2,1)}, u32[]{:S(2)}) copy-start(bf16[768,1,1,512]{0,3,2,1:T(8,128)(2,1)} %fusion.89) | copy-start | bytes 2359300
where the time goes:
time: 141 us; the launch traced here: 140 us
  local copies, waits for them, and re-layouts  41.2 us (29%)
  other arithmetic  38.1 us (27%)
  matrix products  35.5 us (25%)
  starting transfers between devices  20.7 us (15%)
  blocking collectives  4.08 us (3%)
    another operation x7, other arithmetic, skin_block(): return jnp.stack(positions, axis=1).astype(jnp.bfloat16)  28.9 us
    dot_general x4, matrix products, skin_block(): jnp.einsum('mjr,jv->mrv', joint_poses, weight_block, preferred_element_ty...  26.8 us
    another operation x1, local copies, waits for them, and re-layouts, per_device(): return jnp.stack(outputs, axis=1)  16.5 us
    ppermute x6, starting transfers between devices, passed_along(): return lax.ppermute(block, axis, route)  16.5 us
    add x2, local copies, waits for them, and re-layouts, skin_block(): shaped = shaped + template_block.reshape(1, -1).astype(jnp.float32)  12.1 us
    dot_general x4, matrix products, skin_block(): lax.dot_general(coefficients, flattened, (((0,), (0,)), ((), ())), prefer...  8.62 us
    another operation x1, other arithmetic, per_device(): return jnp.stack(outputs, axis=1)  6.69 us
    slice x3, local copies, waits for them, and re-layouts, per_device(): member[slot_index]  5.87 us
  transfers between devices with their start and end apart: 7, of which 0 were waited for; matrix products, arithmetic and copies ran while one was open for 46% of the time, Pallas kernels for 0%

commit v1 on v0

v1 whole, which is shorter than its diff:
```python
import functools

import jax
import jax.numpy as jnp
from jax import lax
from jax.experimental import pallas as pl
from jax.experimental.pallas import tpu as pltpu
from jax.sharding import PartitionSpec as P

MESH = pl.DeviceIdType.MESH
F32 = jnp.float32
BF16 = jnp.bfloat16
K, J, VB, R, STEPS = 120, 24, 512, 768, 4
CHUNK = 128
CHUNKS = R // CHUNK
HALF = VB // 2
PIECES = 5
ROW_GAP = 33


def gather_kernel(
    n_blk,
    coef_ref, tr_ref, bas_ref, tem_ref, wei_ref,
    y_ref, c_ref, w_ref, x_ref, tm_ref,
    got, weights, coef, norm, zs,
    t_send, t_recv, b_send, b_recv, f_send, f_recv, local,
):
    blk = lax.axis_index("blk")
    me = lax.axis_index("batch")
    core = lax.rem(me, 2)
    hi = me // 2
    odd = lax.rem(blk, 2)
    sibling = hi * 2 + (1 - core)
    across = (1 - hi) * 2 + core
    diagonal = (1 - hi) * 2 + (1 - core)
    peers = (sibling, across, diagonal)
    up = lax.rem(blk + 2, n_blk)
    down = lax.rem(blk + n_blk - 2, n_blk)
    beside = blk + 1 - 2 * odd
    half = pl.ds(pl.multiple_of(core * HALF, HALF), HALF)

    own = [
        pltpu.make_async_copy(tr_ref.at[:, :, pl.ds(pl.multiple_of(me * R, R), R)], got.at[0], local.at[0]),
        pltpu.make_async_copy(coef_ref, coef, local.at[1]),
        pltpu.make_async_copy(bas_ref, x_ref.at[0], local.at[2]),
        pltpu.make_async_copy(wei_ref, weights.at[0], local.at[3]),
        pltpu.make_async_copy(tem_ref, tm_ref.at[0], local.at[4]),
    ]
    for copy in own:
        copy.start()

    barrier = pltpu.get_barrier_semaphore()
    for target in (
        (blk, sibling), (blk, across), (blk, diagonal), (beside, across), (up, me), (down, me),
    ):
        pl.semaphore_signal(barrier, inc=1, device_id=target, device_id_type=MESH)
    pl.semaphore_wait(barrier, 6)

    def remote(src, dst, send, recv, target):
        return pltpu.make_async_remote_copy(
            src_ref=src, dst_ref=dst, send_sem=send, recv_sem=recv, device_id=target, device_id_type=MESH
        )

    def slot_parts(slot, span):
        return [x_ref.at[slot, e, :, span] for e in range(3)] + [
            weights.at[slot, :, span], tm_ref.at[slot, :, span],
        ]

    def own_parts(span):
        return [bas_ref.at[e, :, span] for e in range(3)] + [wei_ref.at[:, span], tem_ref.at[:, span]]

    first = [
        remote(s, d, b_send.at[0, p], b_recv.at[1, p], (beside, across))
        for p, (s, d) in enumerate(zip(own_parts(half), slot_parts(1, half)))
    ]
    upward = [
        remote(s, d, b_send.at[1, p], b_recv.at[2, p], (up, me))
        for p, (s, d) in enumerate(zip(own_parts(half), slot_parts(2, half)))
    ]
    third = 3 - 2 * odd
    sideways = [
        remote(s, d, b_send.at[2, p], b_recv.at[third, p], (beside, across))
        for p, (s, d) in enumerate(zip(slot_parts(2, half), slot_parts(third, half)))
    ]
    again = [
        remote(s, d, b_send.at[3, p], b_recv.at[3, p], (up, me))
        for p, (s, d) in enumerate(zip(slot_parts(1, half), slot_parts(3, half)))
    ]
    across_core = [
        [
            remote(s, s, f_send.at[slot - 1, p], f_recv.at[slot - 1, p], (blk, sibling))
            for p, s in enumerate(slot_parts(slot, half))
        ]
        for slot in (1, 2, 3)
    ]
    exchange = [
        remote(
            tr_ref.at[:, :, pl.ds(pl.multiple_of(peer * R, R), R)], got.at[r + 1],
            t_send.at[r], t_recv.at[r], (blk, peer),
        )
        for r, peer in enumerate(peers)
    ]
    for copy in exchange:
        copy.start()
    for copy in upward:
        copy.start()

    @pl.when(odd == 0)
    def _():
        for copy in first:
            copy.start()

    zs[...] = jnp.zeros_like(zs)
    norm[...] = jnp.zeros_like(norm)
    w_ref[...] = jnp.zeros_like(w_ref)
    own[1].wait()
    for at in range(CHUNKS):
        part = slice(at * CHUNK, (at + 1) * CHUNK)
        c_ref[part, :] = coef[:, part].astype(F32).T.astype(BF16)

    def spread(slot):
        raw = weights[slot].astype(F32)
        even = (raw / jnp.sum(raw, axis=0, keepdims=True)).astype(BF16).astype(F32)
        for g in range(4):
            norm[g * 8 : g * 8 + 6, :] = even[g * 6 : g * 6 + 6]
        rows = jnp.concatenate(
            [norm[pl.ds(pl.multiple_of(g * 8, 8), 8), :] for g in (me,) + peers], axis=0
        ).astype(BF16)
        for e in range(4):
            w_ref[slot, e, e * 32 : e * 32 + 32, :] = rows

    own[3].wait()
    spread(0)

    for p in range(PIECES):
        upward[p].wait_recv()
        sideways[p].start()
        across_core[1][p].start()
    for p in range(PIECES):
        first[p].wait_recv()
        across_core[0][p].start()

        @pl.when(odd == 0)
        def _(p=p):
            again[p].start()

    own[0].wait()
    for r in range(3):
        exchange[r].wait_recv()
    for m in range(12):
        for r in range(4):
            zs[m // 4, (m % 4) * 32 + r * 8 : (m % 4) * 32 + r * 8 + 6, :] = got[r, m].astype(F32)
    for at in range(CHUNKS):
        for d in range(3):
            y_ref[at, d] = zs[d, :, at * CHUNK : (at + 1) * CHUNK].T.astype(BF16)

    for p in range(PIECES):
        again[p].wait_recv()
        across_core[2][p].start()
    for slot in (1, 2, 3):
        for p in range(PIECES):
            across_core[slot - 1][p].wait_recv()
        spread(slot)

    for k in (2, 4):
        own[k].wait()
    for copy in exchange + upward + sideways + sum(across_core, []):
        copy.wait_send()

    @pl.when(odd == 0)
    def _():
        for copy in first + again:
            copy.wait_send()


def compute_kernel(y_ref, c_ref, w_ref, x_ref, tm_ref, o_ref, shaped, staged):
    at = pl.program_id(0)
    rows = pl.ds(pl.multiple_of(at * CHUNK, CHUNK), CHUNK)
    for s in range(STEPS):
        for vt in range(2):
            span = slice(vt * HALF, (vt + 1) * HALF)
            for e in range(3):
                shaped[vt, e] = jnp.dot(
                    c_ref[rows, :], x_ref[s, e, :, span], preferred_element_type=F32
                ) + tm_ref[s, e : e + 1, span].astype(F32)
            for d in range(3):
                pose = y_ref[at, d]
                total = jnp.dot(pose, w_ref[s, 3, :, span], preferred_element_type=F32)
                for e in range(3):
                    total = total + shaped[vt, e] * jnp.dot(
                        pose, w_ref[s, e, :, span], preferred_element_type=F32
                    )
                for h in range(2):
                    place = (vt * 2 + h) * STEPS + s
                    for c0 in range(0, CHUNK, 8):
                        staged[d, pl.ds(ROW_GAP * c0 + 2 * place, 8, stride=ROW_GAP), :] = total[
                            c0 : c0 + 8, h * 128 : (h + 1) * 128
                        ]
    for c in range(CHUNK):
        for d in range(3):
            low = staged[d, pl.ds(ROW_GAP * c, 8, stride=2), :]
            high = staged[d, pl.ds(ROW_GAP * c + 16, 8, stride=2), :]
            o_ref[c, d] = jnp.concatenate([low, high], axis=0).astype(BF16)


def per_device(n_blk, coefficients, transforms, basis, template, skin_weights):
    any_space = pl.BlockSpec(memory_space=pltpu.HBM)
    vmem = pl.BlockSpec(memory_space=pltpu.VMEM)
    shape = jax.ShapeDtypeStruct
    dma = pltpu.SemaphoreType.DMA
    gathered = pl.pallas_call(
        functools.partial(gather_kernel, n_blk),
        out_shape=[
            shape((CHUNKS, 3, CHUNK, 128), BF16),
            shape((R, K), BF16),
            shape((STEPS, 4, 128, VB), BF16),
            shape((STEPS, 3, K, VB), BF16),
            shape((STEPS, 3, VB), BF16),
        ],
        in_specs=[any_space] * 5,
        out_specs=[vmem] * 5,
        scratch_shapes=[
            pltpu.VMEM((4, 12, 6, R), BF16),
            pltpu.VMEM((STEPS, J, VB), BF16),
            pltpu.VMEM((K, R), BF16),
            pltpu.VMEM((32, VB), F32),
            pltpu.VMEM((3, 128, R), F32),
            dma((3,)), dma((3,)),
            dma((4, PIECES)), dma((4, PIECES)),
            dma((3, PIECES)), dma((3, PIECES)),
            dma((5,)),
        ],
        compiler_params=pltpu.CompilerParams(
            collective_id=0, has_side_effects=True, vmem_limit_bytes=24 * 2**20
        ),
        name="gather",
    )(coefficients, transforms, jnp.transpose(basis, (1, 0, 2)), template, skin_weights)
    posed = pl.pallas_call(
        compute_kernel,
        grid=(CHUNKS,),
        out_shape=shape((R, 3, 16, 128), BF16),
        in_specs=[vmem] * 5,
        out_specs=pl.BlockSpec((CHUNK, 3, 16, 128), lambda i: (i, 0, 0, 0)),
        scratch_shapes=[
            pltpu.VMEM((2, 3, CHUNK, HALF), F32),
            pltpu.VMEM((3, CHUNK * ROW_GAP + 8, 128), F32),
        ],
        compiler_params=pltpu.CompilerParams(vmem_limit_bytes=32 * 2**20),
        cost_estimate=pl.CostEstimate(flops=4 * 10**9, bytes_accessed=14 * 10**6, transcendentals=0),
        name="compute",
    )(*gathered)
    return posed.reshape(R, 3, 4, STEPS, 128).transpose(0, 3, 1, 2, 4).reshape(R, STEPS, 3, VB)


def solution(mesh):
    both = ("blk", "batch")
    return jax.shard_map(
        functools.partial(per_device, mesh.shape["blk"]),
        mesh=mesh,
        in_specs=(P(None, both), P(None, "batch", "blk"), P(None, None, "blk"), P(None, "blk"), P(None, "blk")),
        out_specs=P(both, None, None, None),
        check_vma=False,
    )
```

time: 141 us -> 45.9 us (0.33)
  the two profiles are of different devices: /device:TPU:126 before, /device:TPU:1 now
where the time goes in v1:
time: 45.9 us; the launch traced here: 45.7 us
  Pallas kernels  41.3 us (90%)
  local copies, waits for them, and re-layouts  4.4 us (10%)
    pallas_call x1, Pallas kernels, per_device(): pl.pallas_call(functools.partial(gather_kernel, n_blk), out_shape=[shape(...  26.1 us
    pallas_call x1, Pallas kernels, per_device(): pl.pallas_call(compute_kernel, grid=(CHUNKS,), out_shape=shape((R, 3, 16,...  15.2 us
    unnamed x10, local copies, waits for them, and re-layouts  4.4 us

profile of v1, /device:TPU:1, one launch (start us, length us, event | category | flops | bytes accessed | tf_op | source)
XLA Modules:
  0.0 45.7 jit_solution(1534370971056289996)
XLA Ops:
  0.0 0.0 copy-start
  0.0 1.1 %copy-done = bf16[12,6,3072]{2,1,0:T(8,128)(2,1)S(1)} copy-done((bf16[12,6,3072]{2,1,0:T(8,128)(2,1)S(1)}, bf16[12,6,3072]{2,1,0:T(8,128)(2,1)}, u32[]{:S(2)}) %copy-start) | copy-done | bytes 442392
  1.1 0.0 copy-start.1
  1.1 1.0 %copy-done.1 = bf16[120,3,512]{2,0,1:T(8,128)(2,1)S(1)} copy-done((bf16[120,3,512]{2,0,1:T(8,128)(2,1)S(1)}, bf16[120,3,512]{2,0,1:T(8,128)(2,1)}, u32[]{:S(2)}) %copy-start.1) | copy-done | bytes 368664
  2.1 0.0 copy-start.2
  2.1 0.9 %copy-done.2 = bf16[120,768]{1,0:T(8,128)(2,1)S(1)} copy-done((bf16[120,768]{1,0:T(8,128)(2,1)S(1)}, bf16[120,768]{1,0:T(8,128)(2,1)}, u32[]{:S(2)}) %copy-start.2) | copy-done | bytes 184344
  3.0 0.0 copy-start.3
  3.0 0.7 %copy-done.3 = bf16[24,512]{1,0:T(8,128)(2,1)S(1)} copy-done((bf16[24,512]{1,0:T(8,128)(2,1)S(1)}, bf16[24,512]{1,0:T(8,128)(2,1)}, u32[]{:S(2)}) %copy-start.3) | copy-done | bytes 24600
  3.7 0.0 copy-start.4
  3.7 0.7 %copy-done.4 = bf16[3,512]{1,0:T(4,128)(2,1)S(1)} copy-done((bf16[3,512]{1,0:T(4,128)(2,1)S(1)}, bf16[3,512]{1,0:T(4,128)(2,1)}, u32[]{:S(2)}) %copy-start.4) | copy-done | bytes 3096
  4.4 26.1 %gather.1 = (bf16[6,3,128,128]{3,2,1,0:T(8,128)(2,1)S(1)}, bf16[768,120]{1,0:T(8,128)(2,1)S(1)}, bf16[4,4,128,512]{3,2,1,0:T(8,128)(2,1)S(1)}, bf16[4,3,120,512]...) custom-call(bf16[120,768]{1,0:T(8,128)(2,1)S(1)} %copy-done.2, bf16[12,6,3072]{2,1,0:T(8,128)(2,1)S(1)} %copy-done, ...), custom_call_target="tpu_custom_call" | custom-call | tf_op jit(solution)/shard_map/gather/pallas_call | solution.py:211
  30.5 15.2 %compute.1 = bf16[768,3,16,128]{3,2,1,0:T(8,128)(2,1)} custom-call(bf16[6,3,128,128]{3,2,1,0:T(8,128)(2,1)S(1)} %get-tuple-element.10.y_ref, bf16[768,120]{1,0:T(8,128)(2,1)S(1)} %get-tuple-element.11.c_ref, bf16[4,4,128,512]{3,2,1,0:T(8,128)(2,1)S(1)} %get-tuple-element.12.w_ref, bf16[4,3,120,512]{3,2,1,0:T(8,128)(2,1)S(1)} %get-tuple-element.13.x_ref, ...), custom_call_target="tpu_custom_call" | custom-call | flops 4000000000 | bytes 14000000 | tf_op jit(solution)/shard_map/compute/pallas_call | solution.py:238
Async XLA Ops:
  0.0 1.1 %copy-start = (bf16[12,6,3072]{2,1,0:T(8,128)(2,1)S(1)}, bf16[12,6,3072]{2,1,0:T(8,128)(2,1)}, u32[]{:S(2)}) copy-start(bf16[12,6,3072]{2,1,0:T(8,128)(2,1)} %tr_ref.1) | copy-start | bytes 1327108
  1.1 1.0 %copy-start.1 = (bf16[120,3,512]{2,0,1:T(8,128)(2,1)S(1)}, bf16[120,3,512]{2,0,1:T(8,128)(2,1)}, u32[]{:S(2)}) copy-start(bf16[120,3,512]{2,0,1:T(8,128)(2,1)} %param.7) | copy-start | bytes 1105924
  2.1 0.9 %copy-start.2 = (bf16[120,768]{1,0:T(8,128)(2,1)S(1)}, bf16[120,768]{1,0:T(8,128)(2,1)}, u32[]{:S(2)}) copy-start(bf16[120,768]{1,0:T(8,128)(2,1)} %coef_ref.1) | copy-start | bytes 552964
  3.0 0.7 %copy-start.3 = (bf16[24,512]{1,0:T(8,128)(2,1)S(1)}, bf16[24,512]{1,0:T(8,128)(2,1)}, u32[]{:S(2)}) copy-start(bf16[24,512]{1,0:T(8,128)(2,1)} %wei_ref.1) | copy-start | bytes 73732
  3.7 0.7 %copy-start.4 = (bf16[3,512]{1,0:T(4,128)(2,1)S(1)}, bf16[3,512]{1,0:T(4,128)(2,1)}, u32[]{:S(2)}) copy-start(bf16[3,512]{1,0:T(4,128)(2,1)} %tem_ref.1) | copy-start | bytes 9220

commit v2 on v1

v2 whole, which is shorter than its diff:
```python
import functools

import jax
import jax.numpy as jnp
from jax import lax
from jax.experimental import pallas as pl
from jax.experimental.pallas import tpu as pltpu
from jax.sharding import PartitionSpec as P

MESH = pl.DeviceIdType.MESH
F32 = jnp.float32
BF16 = jnp.bfloat16
K, J, VB, R, STEPS = 120, 24, 512, 768, 4
CHUNK = 128
CHUNKS = R // CHUNK
HALF = VB // 2
PIECES = 5
ROW_GAP = 17
STAGE_ROWS = CHUNK * ROW_GAP + 8
TURNS = 3
TURN = R // TURNS
PACKED = 2
GATHER_VMEM = 20 * 2**20
COMPUTE_VMEM = 20 * 2**20


def spread(raw, norm, groups, out_ref):
    raw = raw.astype(F32)
    even = (raw / jnp.sum(raw, axis=0, keepdims=True)).astype(BF16).astype(F32)
    for g in range(4):
        norm[g * 8 : g * 8 + 6, :] = even[g * 6 : g * 6 + 6]
    rows = jnp.concatenate([norm[pl.ds(pl.multiple_of(g * 8, 8), 8), :] for g in groups], axis=0).astype(BF16)
    for e in range(4):
        out_ref[e, e * 32 : e * 32 + 32, :] = rows


def shape_up(at, s, c_ref, x_ref, tm_ref, shaped):
    rows = pl.ds(pl.multiple_of(at * CHUNK, CHUNK), CHUNK)
    for vt in range(2):
        span = slice(vt * HALF, (vt + 1) * HALF)
        for e in range(3):
            shaped[vt, e] = jnp.dot(
                c_ref[rows, :], x_ref[s, e, :, span], preferred_element_type=F32
            ) + tm_ref[s, e : e + 1, span].astype(F32)


def pose(at, s, y_ref, w_ref, shaped, staged):
    for vt in range(2):
        span = slice(vt * HALF, (vt + 1) * HALF)
        for d in range(3):
            poses = y_ref[at, d]
            total = jnp.dot(poses, w_ref[3, :, span], preferred_element_type=F32)
            for e in range(3):
                total = total + shaped[vt, e] * jnp.dot(poses, w_ref[e, :, span], preferred_element_type=F32)
            for h in range(2):
                place = (vt * 2 + h) * STEPS + s
                for c0 in range(0, CHUNK, 8):
                    staged[d, pl.ds(ROW_GAP * c0 + place, 8, stride=ROW_GAP), :] = total[
                        c0 : c0 + 8, h * 128 : (h + 1) * 128
                    ]


def gather_kernel(
    n_blk,
    coef_ref, tr_ref, bas_ref, tem_ref, wei_ref,
    y_ref, c_ref, w_ref, x_ref, tm_ref, f_ref,
    got, weights, coef, norm, zs, w_now, shaped, shaped_own,
    t_send, t_recv, b_send, b_recv, f_send, f_recv, local,
):
    blk = lax.axis_index("blk")
    me = lax.axis_index("batch")
    core = lax.rem(me, 2)
    hi = me // 2
    odd = lax.rem(blk, 2)
    sibling = hi * 2 + (1 - core)
    across = (1 - hi) * 2 + core
    diagonal = (1 - hi) * 2 + (1 - core)
    peers = (sibling, across, diagonal)
    groups = (me,) + peers
    up = lax.rem(blk + 2, n_blk)
    down = lax.rem(blk + n_blk - 2, n_blk)
    beside = blk + 1 - 2 * odd
    half = pl.ds(pl.multiple_of(core * HALF, HALF), HALF)

    own = [
        pltpu.make_async_copy(coef_ref, coef, local.at[0]),
        pltpu.make_async_copy(bas_ref, x_ref.at[0], local.at[1]),
        pltpu.make_async_copy(wei_ref, weights.at[0], local.at[2]),
        pltpu.make_async_copy(tem_ref, tm_ref.at[0], local.at[3]),
    ]

    def turn_of(device, turn):
        return tr_ref.at[:, :, pl.ds(pl.multiple_of(device * R + turn * TURN, TURN), TURN)]

    kept = [pltpu.make_async_copy(turn_of(me, turn), got.at[turn, 0], local.at[4 + turn]) for turn in range(TURNS)]
    for copy in own + kept:
        copy.start()

    barrier = pltpu.get_barrier_semaphore()
    for target in ((blk, sibling), (blk, across), (blk, diagonal), (beside, across), (down, me)):
        pl.semaphore_signal(barrier, inc=1, device_id=target, device_id_type=MESH)
    pl.semaphore_wait(barrier, 5)

    def remote(src, dst, send, recv, target):
        return pltpu.make_async_remote_copy(
            src_ref=src, dst_ref=dst, send_sem=send, recv_sem=recv, device_id=target, device_id_type=MESH
        )

    def slot_parts(slot, span):
        return [weights.at[slot, :, span], tm_ref.at[slot, :, span]] + [
            x_ref.at[slot, e, :, span] for e in range(3)
        ]

    def own_parts(span):
        return [wei_ref.at[:, span], tem_ref.at[:, span]] + [bas_ref.at[e, :, span] for e in range(3)]

    first = [
        remote(s, d, b_send.at[0, p], b_recv.at[1, p], (beside, across))
        for p, (s, d) in enumerate(zip(own_parts(half), slot_parts(1, half)))
    ]
    upward = [
        remote(s, d, b_send.at[1, p], b_recv.at[2, p], (up, me))
        for p, (s, d) in enumerate(zip(own_parts(half), slot_parts(2, half)))
    ]
    third = 3 - 2 * odd
    sideways = [
        remote(s, d, b_send.at[2, p], b_recv.at[third, p], (beside, across))
        for p, (s, d) in enumerate(zip(slot_parts(2, half), slot_parts(third, half)))
    ]
    again = [
        remote(s, d, b_send.at[3, p], b_recv.at[3, p], (up, me))
        for p, (s, d) in enumerate(zip(slot_parts(1, half), slot_parts(3, half)))
    ]
    across_core = [
        [
            remote(s, s, f_send.at[slot - 1, p], f_recv.at[slot - 1, p], (blk, sibling))
            for p, s in enumerate(slot_parts(slot, half))
        ]
        for slot in (1, 2, 3)
    ]
    exchange = [
        [
            remote(turn_of(peer, turn), got.at[turn, r + 1], t_send.at[r, turn], t_recv.at[r, turn], (blk, peer))
            for r, peer in enumerate(peers)
        ]
        for turn in range(TURNS)
    ]
    for turn in range(TURNS):
        for copy in exchange[turn]:
            copy.start()
    for copy in upward:
        copy.start()

    @pl.when(odd == 0)
    def _():
        for copy in first:
            copy.start()

    zs[...] = jnp.zeros_like(zs)
    norm[...] = jnp.zeros_like(norm)
    w_now[...] = jnp.zeros_like(w_now)
    w_ref[...] = jnp.zeros_like(w_ref)
    own[0].wait()
    for at in range(CHUNKS):
        part = slice(at * CHUNK, (at + 1) * CHUNK)
        c_ref[part, :] = coef[:, part].astype(F32).T.astype(BF16)
    for k in (1, 2, 3):
        own[k].wait()
    spread(weights[0], norm, groups, w_now)

    parts = TURN // CHUNK
    for at in range(CHUNKS):
        shape_up(at, 0, c_ref, x_ref, tm_ref, shaped_own.at[at])

    def arrive(turn):
        kept[turn].wait()
        for copy in exchange[turn]:
            copy.wait_recv()
        for m in range(12):
            for r in range(4):
                row = (m % 4) * 32 + r * 8
                zs[m // 4, row : row + 6, :] = got[turn, r, m].astype(F32)
        for part in range(parts):
            for d in range(3):
                y_ref[turn * parts + part, d] = zs[d, :, part * CHUNK : (part + 1) * CHUNK].T.astype(BF16)

    def block(s, turn):
        for part in range(parts):
            at = turn * parts + part
            if s == 0:
                mine = shaped_own.at[at]
            else:
                mine = shaped.at[part]
                shape_up(at, s, c_ref, x_ref, tm_ref, mine)
            pose(at, s, y_ref, w_now, mine, f_ref.at[at])

    late = blk < 2

    def hand_slot_2(pieces):
        for p in pieces:
            upward[p].wait_recv()
            sideways[p].start()
            across_core[1][p].start()

    def hand_slot_1(pieces):
        for p in pieces:
            first[p].wait_recv()
            across_core[0][p].start()

            @pl.when(odd == 0)
            def _(p=p):
                again[p].start()

    def hand_slot_3(pieces):
        for p in pieces:
            again[p].wait_recv()
            across_core[2][p].start()

    arrive(0)
    block(0, 0)
    pl.when(jnp.logical_not(late))(lambda: hand_slot_2((0, 1, 2)))
    arrive(1)
    block(0, 1)
    pl.when(jnp.logical_not(late))(lambda: hand_slot_2((3, 4)))
    arrive(2)
    block(0, 2)
    pl.when(late)(lambda: hand_slot_2(range(PIECES)))

    for p in range(PIECES):
        across_core[1][p].wait_recv()
    spread(weights[2], norm, groups, w_now)
    block(2, 0)
    hand_slot_1((0, 1, 2, 3))
    block(2, 1)
    hand_slot_1((4,))
    block(2, 2)

    for p in range(PIECES):
        across_core[0][p].wait_recv()
    spread(weights[1], norm, groups, w_now)
    block(1, 0)
    block(1, 1)
    hand_slot_3((0, 1, 2))
    block(1, 2)
    hand_slot_3((3, 4))
    for p in range(PIECES):
        across_core[2][p].wait_recv()
    spread(weights[3], norm, groups, w_ref)

    for copy in sum(exchange, []) + upward + sideways + sum(across_core, []):
        copy.wait_send()

    @pl.when(odd == 0)
    def _():
        for copy in first + again:
            copy.wait_send()


def compute_kernel(y_ref, c_ref, w_ref, x_ref, tm_ref, _, o_ref, f_ref, *scratch):
    for part in range(PACKED):
        at = pl.program_id(0) * PACKED + part
        shaped = scratch[part]
        shape_up(at, 3, c_ref, x_ref, tm_ref, shaped)
        pose(at, 3, y_ref, w_ref, shaped, f_ref.at[at])
        for c in range(CHUNK):
            for d in range(3):
                o_ref[part * CHUNK + c, d] = f_ref[at, d, pl.ds(ROW_GAP * c, 16), :].astype(BF16)


def per_device(n_blk, coefficients, transforms, basis, template, skin_weights):
    hbm = pl.BlockSpec(memory_space=pltpu.HBM)
    vmem = pl.BlockSpec(memory_space=pltpu.VMEM)
    shape = jax.ShapeDtypeStruct
    dma = pltpu.SemaphoreType.DMA
    gathered = pl.pallas_call(
        functools.partial(gather_kernel, n_blk),
        out_shape=[
            shape((CHUNKS, 3, CHUNK, 128), BF16),
            shape((R, K), BF16),
            shape((4, 128, VB), BF16),
            shape((STEPS, 3, K, VB), BF16),
            shape((STEPS, 3, VB), BF16),
            shape((CHUNKS, 3, STAGE_ROWS, 128), F32),
        ],
        in_specs=[hbm] * 5,
        out_specs=[vmem] * 6,
        scratch_shapes=[
            pltpu.VMEM((TURNS, 4, 12, 6, TURN), BF16),
            pltpu.VMEM((STEPS, J, VB), BF16),
            pltpu.VMEM((K, R), BF16),
            pltpu.VMEM((32, VB), F32),
            pltpu.VMEM((3, 128, TURN), F32),
            pltpu.VMEM((4, 128, VB), BF16),
            pltpu.VMEM((TURN // CHUNK, 2, 3, CHUNK, HALF), F32),
            pltpu.VMEM((CHUNKS, 2, 3, CHUNK, HALF), F32),
            dma((3, TURNS)), dma((3, TURNS)),
            dma((4, PIECES)), dma((4, PIECES)),
            dma((3, PIECES)), dma((3, PIECES)),
            dma((4 + TURNS,)),
        ],
        compiler_params=pltpu.CompilerParams(
            collective_id=0, has_side_effects=True, vmem_limit_bytes=GATHER_VMEM
        ),
        cost_estimate=pl.CostEstimate(flops=3 * 10**9, bytes_accessed=2 * 10**6, transcendentals=0),
        name="gather",
    )(*(
        pltpu.with_memory_space_constraint(a, pltpu.HBM)
        for a in (coefficients, transforms, jnp.transpose(basis, (1, 0, 2)), template, skin_weights)
    ))
    posed, _ = pl.pallas_call(
        compute_kernel,
        grid=(CHUNKS // PACKED,),
        out_shape=[shape((R, 3, 16, 128), BF16), gathered[5]],
        input_output_aliases={5: 1},
        in_specs=[vmem] * 6,
        out_specs=[pl.BlockSpec((PACKED * CHUNK, 3, 16, 128), lambda i: (i, 0, 0, 0)), vmem],
        scratch_shapes=[
            pltpu.VMEM((2, 3, CHUNK, HALF), F32),
        ] * PACKED,
        compiler_params=pltpu.CompilerParams(vmem_limit_bytes=COMPUTE_VMEM),
        cost_estimate=pl.CostEstimate(flops=10**9, bytes_accessed=10**7, transcendentals=0),
        name="compute",
    )(*gathered)
    return posed.reshape(R, 3, 4, STEPS, 128).transpose(0, 3, 1, 2, 4).reshape(R, STEPS, 3, VB)


def solution(mesh):
    both = ("blk", "batch")
    return jax.shard_map(
        functools.partial(per_device, mesh.shape["blk"]),
        mesh=mesh,
        in_specs=(P(None, both), P(None, "batch", "blk"), P(None, None, "blk"), P(None, "blk"), P(None, "blk")),
        out_specs=P(both, None, None, None),
        check_vma=False,
    )
```

time: 45.9 us -> 35.1 us (0.76)
  Pallas kernels: 41.3 us -> 35 us
  local copies, waits for them, and re-layouts: 4.4 us -> 0 us
    pallas_call x1, Pallas kernels: 15.2 us -> 6.19 us  [per_device(): pl.pallas_call(compute_kernel, grid=(CHUNKS // PACKED,), out_shape=[shape...]
    unnamed x10 -> x0, local copies, waits for them, and re-layouts: 4.4 us -> none
    pallas_call x1, Pallas kernels: 26.1 us -> 28.8 us  [per_device(): pl.pallas_call(functools.partial(gather_kernel, n_blk), out_shape=[shape(...]
where the time goes in v2:
time: 35.1 us; the launch traced here: 35 us
  Pallas kernels  35 us (100%)
    pallas_call x1, Pallas kernels, per_device(): pl.pallas_call(functools.partial(gather_kernel, n_blk), out_shape=[shape(...  28.8 us
    pallas_call x1, Pallas kernels, per_device(): pl.pallas_call(compute_kernel, grid=(CHUNKS // PACKED,), out_shape=[shape...  6.19 us

profile of v2, /device:TPU:1, one launch (start us, length us, event | category | flops | bytes accessed | tf_op | source)
XLA Modules:
  0.0 35.0 jit_solution(10931601966401142005)
XLA Ops:
  0.0 28.8 %gather.1 = (bf16[6,3,128,128]{3,2,1,0:T(8,128)(2,1)S(1)}, bf16[768,120]{1,0:T(8,128)(2,1)S(1)}, bf16[4,128,512]{2,1,0:T(8,128)(2,1)S(1)}, bf16[4,3,120,512]{3,2...) custom-call(bf16[120,768]{1,0:T(8,128)(2,1)} %coef_ref.1, ...), custom_call_target="tpu_custom_call" | custom-call | flops 3000000000 | bytes 2000000 | tf_op jit(solution)/shard_map/gather/pallas_call | solution.py:275
  28.8 6.2 %compute.1 = (bf16[768,3,16,128]{3,2,1,0:T(8,128)(2,1)}, f32[6,3,2184,128]{3,2,1,0:T(8,128)S(1)}) custom-call(bf16[6,3,128,128]{3,2,1,0:T(8,128)(2,1)S(1)} %get-tuple-element.12.y_ref, bf16[768,120]{1,0:T(8,128)(2,1)S(1)} %get-tuple-element.13.c_ref, bf16[4,128,512]{2,1,0:T(8,128)(2,1)S(1)} %get-tuple-element.14.w_ref, ...), custom_call_target="tpu_custom_call", output_to_operand_aliasing={{1}: (5, {})} | custom-call | flops 1000000000 | bytes 10000000 | tf_op jit(solution)/shard_map/compute/pallas_call | solution.py:310

commit v3 on v2

--- a/solution.py
+++ b/solution.py
@@ -131,13 +131,11 @@
         remote(s, d, b_send.at[3, p], b_recv.at[3, p], (up, me))
         for p, (s, d) in enumerate(zip(slot_parts(1, half), slot_parts(3, half)))
     ]
-    across_core = [
-        [
-            remote(s, s, f_send.at[slot - 1, p], f_recv.at[slot - 1, p], (blk, sibling))
-            for p, s in enumerate(slot_parts(slot, half))
-        ]
-        for slot in (1, 2, 3)
-    ]
+
+    def across_core(slot, p):
+        part = slot_parts(slot, half)[p]
+        return remote(part, part, f_send.at[slot - 1, p], f_recv.at[slot - 1, p], (blk, sibling))
+
     exchange = [
         [
             remote(turn_of(peer, turn), got.at[turn, r + 1], t_send.at[r, turn], t_recv.at[r, turn], (blk, peer))
@@ -187,67 +185,86 @@
     def block(s, turn):
         for part in range(parts):
             at = turn * parts + part
-            if s == 0:
+            if turn_is_own(s):
                 mine = shaped_own.at[at]
             else:
                 mine = shaped.at[part]
                 shape_up(at, s, c_ref, x_ref, tm_ref, mine)
             pose(at, s, y_ref, w_now, mine, f_ref.at[at])
 
+    def turn_is_own(s):
+        return isinstance(s, int)
+
+    even = odd == 0
     late = blk < 2
+    prompt = jnp.logical_not(late)
 
     def hand_slot_2(pieces):
         for p in pieces:
             upward[p].wait_recv()
             sideways[p].start()
-            across_core[1][p].start()
+            across_core(2, p).start()
 
     def hand_slot_1(pieces):
         for p in pieces:
             first[p].wait_recv()
-            across_core[0][p].start()
-
-            @pl.when(odd == 0)
-            def _(p=p):
-                again[p].start()
+            across_core(1, p).start()
+
+    def hand_slot_1_upward(pieces):
+        for p in pieces:
+            first[p].wait_recv()
+            again[p].start()
+            across_core(1, p).start()
 
     def hand_slot_3(pieces):
         for p in pieces:
             again[p].wait_recv()
-            across_core[2][p].start()
-
+            across_core(3, p).start()
+
+    def where(condition, action, pieces):
+        pl.when(condition)(lambda: action(pieces))
+
+    every = range(PIECES)
     arrive(0)
     block(0, 0)
-    pl.when(jnp.logical_not(late))(lambda: hand_slot_2((0, 1, 2)))
+    where(prompt, hand_slot_2, (0, 1, 2))
     arrive(1)
     block(0, 1)
-    pl.when(jnp.logical_not(late))(lambda: hand_slot_2((3, 4)))
+    where(prompt, hand_slot_2, (3, 4))
+    where(odd == 1, hand_slot_1, every)
     arrive(2)
     block(0, 2)
-    pl.when(late)(lambda: hand_slot_2(range(PIECES)))
-
-    for p in range(PIECES):
-        across_core[1][p].wait_recv()
-    spread(weights[2], norm, groups, w_now)
-    block(2, 0)
-    hand_slot_1((0, 1, 2, 3))
-    block(2, 1)
-    hand_slot_1((4,))
-    block(2, 2)
-
-    for p in range(PIECES):
-        across_core[0][p].wait_recv()
-    spread(weights[1], norm, groups, w_now)
-    block(1, 0)
-    block(1, 1)
-    hand_slot_3((0, 1, 2))
-    block(1, 2)
-    hand_slot_3((3, 4))
-    for p in range(PIECES):
-        across_core[2][p].wait_recv()
+    where(jnp.logical_and(late, even), hand_slot_2, every)
+
+    one = 2 - odd
+    for p in every:
+        across_core(one, p).wait_recv()
+    spread(weights[one], norm, groups, w_now)
+    block(one, 0)
+    where(even, hand_slot_1_upward, (0, 1, 2))
+    block(one, 1)
+    where(even, hand_slot_1_upward, (3, 4))
+    where(jnp.logical_and(late, odd == 1), hand_slot_2, (0, 1, 2))
+    block(one, 2)
+    where(jnp.logical_and(late, odd == 1), hand_slot_2, (3, 4))
+
+    two = 1 + odd
+    for p in every:
+        across_core(two, p).wait_recv()
+    spread(weights[two], norm, groups, w_now)
+    late_third = jnp.logical_and(even, blk < 4)
+    block(two, 0)
+    where(jnp.logical_and(odd == 1, prompt), hand_slot_3, every)
+    block(two, 1)
+    where(jnp.logical_and(even, blk >= 4), hand_slot_3, every)
+    block(two, 2)
+    where(jnp.logical_or(late, late_third), hand_slot_3, every)
+    for p in every:
+        across_core(3, p).wait_recv()
     spread(weights[3], norm, groups, w_ref)
 
-    for copy in sum(exchange, []) + upward + sideways + sum(across_core, []):
+    passed = [across_core(slot, p) for slot in (1, 2, 3) for p in every]
+    for copy in sum(exchange, []) + upward + sideways + passed:
         copy.wait_send()
 
     @pl.when(odd == 0)

time: 35.1 us -> 35.4 us (level)
  no operation moved by 1% of the time
where the time goes in v3:
time: 35.4 us; the launch traced here: 35.3 us
  Pallas kernels  35.3 us (100%)
    pallas_call x1, Pallas kernels, per_device(): pl.pallas_call(functools.partial(gather_kernel, n_blk), out_shape=[shape(...  29.1 us
    pallas_call x1, Pallas kernels, per_device(): pl.pallas_call(compute_kernel, grid=(CHUNKS // PACKED,), out_shape=[shape...  6.19 us

profile of v3, /device:TPU:1, one launch (start us, length us, event | category | flops | bytes accessed | tf_op | source)
XLA Modules:
  0.0 35.3 jit_solution(5620525121285375632)
XLA Ops:
  0.0 29.1 %gather.1 = (bf16[6,3,128,128]{3,2,1,0:T(8,128)(2,1)S(1)}, bf16[768,120]{1,0:T(8,128)(2,1)S(1)}, bf16[4,128,512]{2,1,0:T(8,128)(2,1)S(1)}, bf16[4,3,120,512]{3,2...) custom-call(bf16[120,768]{1,0:T(8,128)(2,1)} %coef_ref.1, ...), custom_call_target="tpu_custom_call" | custom-call | flops 3000000000 | bytes 2000000 | tf_op jit(solution)/shard_map/gather/pallas_call | solution.py:292
  29.1 6.2 %compute.1 = (bf16[768,3,16,128]{3,2,1,0:T(8,128)(2,1)}, f32[6,3,2184,128]{3,2,1,0:T(8,128)S(1)}) custom-call(bf16[6,3,128,128]{3,2,1,0:T(8,128)(2,1)S(1)} %get-tuple-element.12.y_ref, bf16[768,120]{1,0:T(8,128)(2,1)S(1)} %get-tuple-element.13.c_ref, bf16[4,128,512]{2,1,0:T(8,128)(2,1)S(1)} %get-tuple-element.14.w_ref, ...), custom_call_target="tpu_custom_call", output_to_operand_aliasing={{1}: (5, {})} | custom-call | flops 1000000000 | bytes 10000000 | tf_op jit(solution)/shard_map/compute/pallas_call | solution.py:327

commit v4 on v3

--- a/solution.py
+++ b/solution.py
@@ -80,6 +80,10 @@
     up = lax.rem(blk + 2, n_blk)
     down = lax.rem(blk + n_blk - 2, n_blk)
     beside = blk + 1 - 2 * odd
+    ahead = lax.rem(blk + 1, n_blk)
+    behind = lax.rem(blk + n_blk - 1, n_blk)
+    to_first = ahead == 0
+    from_last = blk == 0
     half = pl.ds(pl.multiple_of(core * HALF, HALF), HALF)
 
     own = [
@@ -99,7 +103,10 @@
     barrier = pltpu.get_barrier_semaphore()
     for target in ((blk, sibling), (blk, across), (blk, diagonal), (beside, across), (down, me)):
         pl.semaphore_signal(barrier, inc=1, device_id=target, device_id_type=MESH)
-    pl.semaphore_wait(barrier, 5)
+    pl.when(from_last)(
+        lambda: pl.semaphore_signal(barrier, inc=1, device_id=(behind, across), device_id_type=MESH)
+    )
+    pl.semaphore_wait(barrier, 5 + (blk + 1) // n_blk)
 
     def remote(src, dst, send, recv, target):
         return pltpu.make_async_remote_copy(
@@ -130,6 +137,10 @@
     again = [
         remote(s, d, b_send.at[3, p], b_recv.at[3, p], (up, me))
         for p, (s, d) in enumerate(zip(slot_parts(1, half), slot_parts(3, half)))
+    ]
+    direct = [
+        remote(s, d, b_send.at[0, p], b_recv.at[3, p], (ahead, across))
+        for p, (s, d) in enumerate(zip(slot_parts(2, half), slot_parts(3, half)))
     ]
 
     def across_core(slot, p):
@@ -202,6 +213,7 @@
     def hand_slot_2(pieces):
         for p in pieces:
             upward[p].wait_recv()
+            pl.when(to_first)(direct[p].start)
             sideways[p].start()
             across_core(2, p).start()
 
@@ -213,7 +225,7 @@
     def hand_slot_1_upward(pieces):
         for p in pieces:
             first[p].wait_recv()
-            again[p].start()
+            pl.when(up != 0)(again[p].start)
             across_core(1, p).start()
 
     def hand_slot_3(pieces):
@@ -244,21 +256,20 @@
     where(even, hand_slot_1_upward, (0, 1, 2))
     block(one, 1)
     where(even, hand_slot_1_upward, (3, 4))
-    where(jnp.logical_and(late, odd == 1), hand_slot_2, (0, 1, 2))
+    where(jnp.logical_and(late, odd == 1), hand_slot_2, every)
     block(one, 2)
-    where(jnp.logical_and(late, odd == 1), hand_slot_2, (3, 4))
 
     two = 1 + odd
     for p in every:
         across_core(two, p).wait_recv()
     spread(weights[two], norm, groups, w_now)
-    late_third = jnp.logical_and(even, blk < 4)
+    last_third = jnp.logical_or(blk == 1, blk == 2)
     block(two, 0)
     where(jnp.logical_and(odd == 1, prompt), hand_slot_3, every)
     block(two, 1)
-    where(jnp.logical_and(even, blk >= 4), hand_slot_3, every)
+    where(jnp.logical_and(even, blk != 2), hand_slot_3, every)
     block(two, 2)
-    where(jnp.logical_or(late, late_third), hand_slot_3, every)
+    where(last_third, hand_slot_3, every)
     for p in every:
         across_core(3, p).wait_recv()
     spread(weights[3], norm, groups, w_ref)
@@ -269,7 +280,17 @@
 
     @pl.when(odd == 0)
     def _():
-        for copy in first + again:
+        for copy in first:
+            copy.wait_send()
+
+    @pl.when(jnp.logical_and(odd == 0, up != 0))
+    def _():
+        for copy in again:
+            copy.wait_send()
+
+    @pl.when(to_first)
+    def _():
+        for copy in direct:
             copy.wait_send()
 
 

time: 35.4 us -> 34.2 us (0.966)
  Pallas kernels: 35.3 us -> 34.1 us
    pallas_call x1, Pallas kernels: 29.1 us -> 27.9 us  [per_device(): pl.pallas_call(functools.partial(gather_kernel, n_blk), out_shape=[shape(...]
where the time goes in v4:
time: 34.2 us; the launch traced here: 34.1 us
  Pallas kernels  34.1 us (100%)
    pallas_call x1, Pallas kernels, per_device(): pl.pallas_call(functools.partial(gather_kernel, n_blk), out_shape=[shape(...  27.9 us
    pallas_call x1, Pallas kernels, per_device(): pl.pallas_call(compute_kernel, grid=(CHUNKS // PACKED,), out_shape=[shape...  6.19 us

profile of v4, /device:TPU:1, one launch (start us, length us, event | category | flops | bytes accessed | tf_op | source)
XLA Modules:
  0.0 34.1 jit_solution(8016646123143796275)
XLA Ops:
  0.0 27.9 %gather.1 = (bf16[6,3,128,128]{3,2,1,0:T(8,128)(2,1)S(1)}, bf16[768,120]{1,0:T(8,128)(2,1)S(1)}, bf16[4,128,512]{2,1,0:T(8,128)(2,1)S(1)}, bf16[4,3,120,512]{3,2...) custom-call(bf16[120,768]{1,0:T(8,128)(2,1)} %coef_ref.1, ...), custom_call_target="tpu_custom_call" | custom-call | flops 3000000000 | bytes 2000000 | tf_op jit(solution)/shard_map/gather/pallas_call | solution.py:313
  27.9 6.2 %compute.1 = (bf16[768,3,16,128]{3,2,1,0:T(8,128)(2,1)}, f32[6,3,2184,128]{3,2,1,0:T(8,128)S(1)}) custom-call(bf16[6,3,128,128]{3,2,1,0:T(8,128)(2,1)S(1)} %get-tuple-element.12.y_ref, bf16[768,120]{1,0:T(8,128)(2,1)S(1)} %get-tuple-element.13.c_ref, bf16[4,128,512]{2,1,0:T(8,128)(2,1)S(1)} %get-tuple-element.14.w_ref, ...), custom_call_target="tpu_custom_call", output_to_operand_aliasing={{1}: (5, {})} | custom-call | flops 1000000000 | bytes 10000000 | tf_op jit(solution)/shard_map/compute/pallas_call | solution.py:348

commit v5 on v4

--- a/solution.py
+++ b/solution.py
@@ -254,9 +254,10 @@
     spread(weights[one], norm, groups, w_now)
     block(one, 0)
     where(even, hand_slot_1_upward, (0, 1, 2))
+    where(blk == 1, hand_slot_2, (0, 1, 2))
     block(one, 1)
     where(even, hand_slot_1_upward, (3, 4))
-    where(jnp.logical_and(late, odd == 1), hand_slot_2, every)
+    where(blk == 1, hand_slot_2, (3, 4))
     block(one, 2)
 
     two = 1 + odd

time: 34.2 us -> 33.3 us (0.974)
  Pallas kernels: 34.1 us -> 33.2 us
    pallas_call x1, Pallas kernels: 27.9 us -> 27 us  [per_device(): pl.pallas_call(functools.partial(gather_kernel, n_blk), out_shape=[shape(...]
where the time goes in v5:
time: 33.3 us; the launch traced here: 33.2 us
  Pallas kernels  33.2 us (100%)
    pallas_call x1, Pallas kernels, per_device(): pl.pallas_call(functools.partial(gather_kernel, n_blk), out_shape=[shape(...  27 us
    pallas_call x1, Pallas kernels, per_device(): pl.pallas_call(compute_kernel, grid=(CHUNKS // PACKED,), out_shape=[shape...  6.19 us

profile of v5, /device:TPU:1, one launch (start us, length us, event | category | flops | bytes accessed | tf_op | source)
XLA Modules:
  0.0 33.2 jit_solution(5218602475295890596)
XLA Ops:
  0.0 27.0 %gather.1 = (bf16[6,3,128,128]{3,2,1,0:T(8,128)(2,1)S(1)}, bf16[768,120]{1,0:T(8,128)(2,1)S(1)}, bf16[4,128,512]{2,1,0:T(8,128)(2,1)S(1)}, bf16[4,3,120,512]{3,2...) custom-call(bf16[120,768]{1,0:T(8,128)(2,1)} %coef_ref.1, ...), custom_call_target="tpu_custom_call" | custom-call | flops 3000000000 | bytes 2000000 | tf_op jit(solution)/shard_map/gather/pallas_call | solution.py:314
  27.0 6.2 %compute.1 = (bf16[768,3,16,128]{3,2,1,0:T(8,128)(2,1)}, f32[6,3,2184,128]{3,2,1,0:T(8,128)S(1)}) custom-call(bf16[6,3,128,128]{3,2,1,0:T(8,128)(2,1)S(1)} %get-tuple-element.12.y_ref, bf16[768,120]{1,0:T(8,128)(2,1)S(1)} %get-tuple-element.13.c_ref, bf16[4,128,512]{2,1,0:T(8,128)(2,1)S(1)} %get-tuple-element.14.w_ref, ...), custom_call_target="tpu_custom_call", output_to_operand_aliasing={{1}: (5, {})} | custom-call | flops 1000000000 | bytes 10000000 | tf_op jit(solution)/shard_map/compute/pallas_call | solution.py:349

commit v6 on v5

--- a/solution.py
+++ b/solution.py
@@ -211,11 +211,21 @@
     prompt = jnp.logical_not(late)
 
     def hand_slot_2(pieces):
-        for p in pieces:
-            upward[p].wait_recv()
-            pl.when(to_first)(direct[p].start)
-            sideways[p].start()
-            across_core(2, p).start()
+        @pl.when(to_first)
+        def _():
+            for p in pieces:
+                upward[p].wait_recv()
+                direct[p].start()
+            for p in pieces:
+                sideways[p].start()
+                across_core(2, p).start()
+
+        @pl.when(jnp.logical_not(to_first))
+        def _():
+            for p in pieces:
+                upward[p].wait_recv()
+                sideways[p].start()
+                across_core(2, p).start()
 
     def hand_slot_1(pieces):
         for p in pieces:
@@ -252,11 +262,14 @@
     for p in every:
         across_core(one, p).wait_recv()
     spread(weights[one], norm, groups, w_now)
+    where(from_last, hand_slot_1_upward, (0, 1, 2))
     block(one, 0)
-    where(even, hand_slot_1_upward, (0, 1, 2))
+    where(jnp.logical_and(even, prompt), hand_slot_1_upward, (0, 1, 2))
+    where(from_last, hand_slot_1_upward, (3,))
     where(blk == 1, hand_slot_2, (0, 1, 2))
     block(one, 1)
-    where(even, hand_slot_1_upward, (3, 4))
+    where(jnp.logical_and(even, prompt), hand_slot_1_upward, (3, 4))
+    where(from_last, hand_slot_1_upward, (4,))
     where(blk == 1, hand_slot_2, (3, 4))
     block(one, 2)
 

time: 33.3 us -> 34 us (1.021)
  Pallas kernels: 33.2 us -> 33.9 us
    pallas_call x1, Pallas kernels: 27 us -> 27.8 us  [per_device(): pl.pallas_call(functools.partial(gather_kernel, n_blk), out_shape=[shape(...]
where the time goes in v6:
time: 34 us
  Pallas kernels  33.9 us (100%)
    pallas_call x1, Pallas kernels, per_device(): pl.pallas_call(functools.partial(gather_kernel, n_blk), out_shape=[shape(...  27.8 us
    pallas_call x1, Pallas kernels, per_device(): pl.pallas_call(compute_kernel, grid=(CHUNKS // PACKED,), out_shape=[shape...  6.19 us

profile of v6, /device:TPU:1, one launch (start us, length us, event | category | flops | bytes accessed | tf_op | source)
XLA Modules:
  0.0 34.0 jit_solution(18334955927151057345)
XLA Ops:
  0.0 27.8 %gather.1 = (bf16[6,3,128,128]{3,2,1,0:T(8,128)(2,1)S(1)}, bf16[768,120]{1,0:T(8,128)(2,1)S(1)}, bf16[4,128,512]{2,1,0:T(8,128)(2,1)S(1)}, bf16[4,3,120,512]{3,2...) custom-call(bf16[120,768]{1,0:T(8,128)(2,1)} %coef_ref.1, ...), custom_call_target="tpu_custom_call" | custom-call | flops 3000000000 | bytes 2000000 | tf_op jit(solution)/shard_map/gather/pallas_call | solution.py:327
  27.8 6.2 %compute.1 = (bf16[768,3,16,128]{3,2,1,0:T(8,128)(2,1)}, f32[6,3,2184,128]{3,2,1,0:T(8,128)S(1)}) custom-call(bf16[6,3,128,128]{3,2,1,0:T(8,128)(2,1)S(1)} %get-tuple-element.12.y_ref, bf16[768,120]{1,0:T(8,128)(2,1)S(1)} %get-tuple-element.13.c_ref, bf16[4,128,512]{2,1,0:T(8,128)(2,1)S(1)} %get-tuple-element.14.w_ref, ...), custom_call_target="tpu_custom_call", output_to_operand_aliasing={{1}: (5, {})} | custom-call | flops 1000000000 | bytes 10000000 | tf_op jit(solution)/shard_map/compute/pallas_call | solution.py:362
